TPU v7x, 32 devices: a whole 2x2x4 slice. The times are simulated.
32 devices in a mesh: row: 4 (over x, core), col: 8 (over z, y).
Axes of the slice: x: 2, y: 2, z: 4, core: 2. Of those that a mesh axis runs over, the one named last changes fastest.
Arguments:
- left_factor: bfloat16 [4096, 2048], P('row', 'col'), may hold values from -6 to 6
- right_factor: bfloat16 [2048, 8192], P('row', 'col'), may hold values from -0.125 to 0.125
- matrix: float32 [4096, 8192], P('row', 'col'), may hold values from -6 to 6
- pivot_scale: float32 [2048], replicated, may hold values from 0.25 to 1.75
Outputs:
- updated: float32 [4096, 8192], P('row', 'col')
All inputs are finite; a program needn't handle non-finite values.
Results may differ from a plain program's by a relative error of at most 0.0003.
Values may be sent and summed in bfloat16 or wider, within the bound.
A program may use at most 128 MiB of HBM per device.

v0:
```python
import jax
import jax.numpy as jnp
from jax import lax
from jax.sharding import PartitionSpec as P


def taken_in(shard, axis, dim, absorb, state):
    everything = jax.tree.map(lambda a: lax.all_gather(a, axis, axis=dim, tiled=True), shard)
    return absorb(state, everything, jnp.int32(0))


def join_panel(carry, left_panel, right_panel):
    return carry + jnp.dot(left_panel, right_panel, preferred_element_type=jnp.float32)


def per_device(left_factor, right_factor, matrix, pivot_scale):
    share = left_factor.shape[1]
    part_scale = lax.dynamic_slice_in_dim(pivot_scale, lax.axis_index("col") * share, share)
    scaled_left = (left_factor.astype(jnp.float32) * part_scale).astype(jnp.bfloat16)
    begin = jnp.zeros((left_factor.shape[0], right_factor.shape[1]), jnp.float32)
    left_line = lax.all_gather(scaled_left, "col", axis=1, tiled=True)

    def take_rows(carry, piece, start):
        left_piece = lax.dynamic_slice_in_dim(left_line, start, piece.shape[0], axis=1)
        return join_panel(carry, left_piece, piece)

    total = taken_in(right_factor, "row", 0, take_rows, begin)
    updated = matrix - total
    row_power = lax.psum(jnp.sum(updated * updated, axis=1), "col")
    updated = (
        updated * lax.rsqrt(row_power / (updated.shape[1] * lax.axis_size("col")) + 1e-06)[:, None]
    )
    return updated


def solution(mesh):
    in_specs = (P("row", "col"), P("row", "col"), P("row", "col"), P())
    out_specs = P("row", "col")
    return jax.shard_map(
        per_device, mesh=mesh, in_specs=in_specs, out_specs=out_specs, check_vma=False
    )
```

profile of v0, /device:TPU:0, one launch (start us, length us, event | category | flops | bytes accessed | tf_op | source)
XLA Modules:
  0.0 169.9 jit_solution(15891152812098854044)
XLA Ops:
  6.5 0.0 all-gather.5.cloned.1.call-start
  6.5 0.7 all-gather.5.cloned.1.call-update
  7.3 0.0 all-gather.3.cloned.1.call-start
  7.3 0.8 dynamic_slice.3
  8.1 2.0 %multiply_convert_fusion = bf16[1024,256]{1,0:T(8,128)(2,1)} fusion(bf16[1024,256]{1,0:T(8,128)(2,1)} %param.4, f32[256]{0:T(256)S(1)} %dynamic_slice.3), kind=kLoop, calls=%fused_computation.3 | loop fusion | flops 786432 | bytes 1049600 | tf_op jit(solution)/shard_map/convert_element_type | solution.py:19
  10.1 0.0 all-gather.3.cloned.1.call-update
  10.1 5.3 %copy.5 = f32[1024,1024]{0,1:T(8,128)} copy(f32[1024,1024]{1,0:T(8,128)} %param.6) | data formatting | bytes 8388608 | tf_op args[2]
  15.4 30.7 %all-gather.5.cloned.1.call-done = bf16[2048,1024]{1,0:T(8,128)(2,1)} async-done(((bf16[512,1024]{1,0:T(8,128)(2,1)}), bf16[2048,1024]{1,0:T(8,128)(2,1)}) %all-gather.5.cloned.1.call-update) | async-done | bytes 4194320 | tf_op jit(solution)/shard_map/all_gather | solution.py:8
  46.1 76.7 %all-gather.3.cloned.1.call-done = bf16[1024,2048]{1,0:T(8,128)(2,1)} async-done(((bf16[1024,256]{1,0:T(8,128)(2,1)}), bf16[1024,2048]{1,0:T(8,128)(2,1)}) %all-gather.3.cloned.1.call-update) | async-done | bytes 4194320 | tf_op jit(solution)/shard_map/all_gather | solution.py:21
  122.8 11.3 %multiply_reduce_fusion = (f32[1024]{0:T(1024)S(1)}, f32[1024,1024]{0,1:T(8,128)}) fusion(f32[1024,1024]{0,1:T(8,128)} %copy.5, bf16[1024,2048]{1,0:T(8,128)(2,1)} %all-gather.3.cloned.1.call-done, bf16[2048,1024]{1,0:T(8,128)(2,1)} %all-gather.5.cloned.1.call-done), kind=kOutput, calls=%fused_computation | convolution fusion | flops 4298112000 | bytes 16781312 | tf_op jit(solution)/shard_map/dot_general | solution.py:13
  134.1 18.6 %psum.7 = f32[1024]{0:T(1024)S(1)} all-reduce(f32[1024]{0:T(1024)S(1)} %get-tuple-element.5), channel_id=1, replica_groups=mesh['row'=4,'col'=8] {'col'}, use_global_device_ids=true, to_apply=%region_1.0 | all-reduce | flops 1024 | bytes 8192 | tf_op jit(solution)/shard_map/psum | solution.py:29
  152.7 5.0 %broadcast_multiply_fusion = f32[1024,1024]{0,1:T(8,128)} fusion(f32[1024,1024]{0,1:T(8,128)} %get-tuple-element.6, f32[1024]{0:T(1024)S(1)} %add_rsqrt_fusion), kind=kLoop, calls=%fused_computation.1 | loop fusion | flops 1048576 | bytes 8392704 | tf_op jit(solution)/shard_map/mul | solution.py:31
  157.7 5.3 %copy.6 = f32[1024,1024]{1,0:T(8,128)} copy(f32[1024,1024]{0,1:T(8,128)} %broadcast_multiply_fusion) | data formatting | bytes 8388608 | tf_op jit(solution)/shard_map/mul | solution.py:31
  (1 shorter events, 0.0 us)
Async XLA Ops:
  6.5 39.6 %all-gather.5.cloned.1.call-start = ((), (), s32[]{:S(2)}) async-start(), calls=%async_computation.1 | async-start | bytes 5242880 | tf_op jit(solution)/shard_map/all_gather | solution.py:8
  7.3 115.6 %all-gather.3.cloned.1.call-start = ((), (), s32[]{:S(2)}) async-start(), calls=%async_computation | async-start | bytes 4718592 | tf_op jit(solution)/shard_map/all_gather | solution.py:21
Sparse Core Ops, SparseCore 0:
  8.9 37.1 all-gather.4
  48.1 74.6 all-gather.2
where the time goes:
time: 170 us
  waiting for transfers between devices  108 us (64%)
  blocking collectives  18.6 us (11%)
  between operations  13.4 us (8%)
  local copies, waits for them, and re-layouts  11.4 us (7%)
  matrix products  11.3 us (7%)
  other arithmetic  6.98 us (4%)
    all_gather x1, waiting for transfers between devices, per_device(): left_line = lax.all_gather(scaled_left, 'col', axis=1, tiled=True)  76.7 us
    all_gather x1, waiting for transfers between devices, taken_in(): lax.all_gather(a, axis, axis=dim, tiled=True)  30.7 us
    psum x1, blocking collectives, per_device(): row_power = lax.psum(jnp.sum(updated * updated, axis=1), 'col')  18.6 us
    dot_general x1, matrix products, join_panel(): jnp.dot(left_panel, right_panel, preferred_element_type=jnp.float32)  11.3 us
    unnamed x1, local copies, waits for them, and re-layouts  5.35 us
    mul x1, local copies, waits for them, and re-layouts, per_device(): updated * lax.rsqrt(row_power / (updated.shape[1] * lax.axis_size('col'))...  5.34 us
    mul x1, other arithmetic, per_device(): updated * lax.rsqrt(row_power / (updated.shape[1] * lax.axis_size('col'))...  4.98 us
  transfers between devices with their start and end apart: 2, of which 2 were waited for; matrix products, arithmetic and copies ran while one was open for 5% of the time, Pallas kernels for 0%

commit v1 on v0

--- a/solution.py
+++ b/solution.py
@@ -18,7 +18,7 @@
     part_scale = lax.dynamic_slice_in_dim(pivot_scale, lax.axis_index("col") * share, share)
     scaled_left = (left_factor.astype(jnp.float32) * part_scale).astype(jnp.bfloat16)
     begin = jnp.zeros((left_factor.shape[0], right_factor.shape[1]), jnp.float32)
-    left_line = lax.all_gather(scaled_left, "col", axis=1, tiled=True)
+    left_line = jnp.concatenate(lax.all_gather(scaled_left, "col"), axis=1)
 
     def take_rows(carry, piece, start):
         left_piece = lax.dynamic_slice_in_dim(left_line, start, piece.shape[0], axis=1)

time: 170 us -> 170 us (level)
  waiting for transfers between devices: 108 us -> 98.4 us
  local copies, waits for them, and re-layouts: 11.4 us -> 17.9 us
  blocking collectives: 18.6 us -> 21.3 us
    all_gather x1, waiting for transfers between devices: 76.7 us -> 69.6 us  [per_device(): left_line = jnp.concatenate(lax.all_gather(scaled_left, 'col'), axis=1)]
    reshape x0 -> x1, local copies, waits for them, and re-layouts: none -> 6.49 us  [per_device(): left_line = jnp.concatenate(lax.all_gather(scaled_left, 'col'), axis=1)]
    psum x1, blocking collectives: 18.6 us -> 21.3 us  [per_device(): row_power = lax.psum(jnp.sum(updated * updated, axis=1), 'col')]
    all_gather x1, waiting for transfers between devices: 30.7 us -> 28.1 us  [taken_in(): lax.all_gather(a, axis, axis=dim, tiled=True)]
  transfers between devices with their start and end apart: 2 -> 2, of which waited for: 2 -> 2; matrix products, arithmetic and copies ran while one was open for 5% -> 7% of each run, Pallas kernels for 0% -> 0%
where the time goes in v1:
time: 170 us; the launch traced here: 169 us
  waiting for transfers between devices  98.4 us (58%)
  blocking collectives  21.3 us (13%)
  local copies, waits for them, and re-layouts  17.9 us (11%)
  between operations  13.4 us (8%)
  matrix products  11.3 us (7%)
  other arithmetic  6.98 us (4%)
    all_gather x1, waiting for transfers between devices, per_device(): left_line = jnp.concatenate(lax.all_gather(scaled_left, 'col'), axis=1)  69.6 us
    all_gather x1, waiting for transfers between devices, taken_in(): lax.all_gather(a, axis, axis=dim, tiled=True)  28.1 us
    psum x1, blocking collectives, per_device(): row_power = lax.psum(jnp.sum(updated * updated, axis=1), 'col')  21.3 us
    dot_general x1, matrix products, join_panel(): jnp.dot(left_panel, right_panel, preferred_element_type=jnp.float32)  11.3 us
    reshape x1, local copies, waits for them, and re-layouts, per_device(): left_line = jnp.concatenate(lax.all_gather(scaled_left, 'col'), axis=1)  6.49 us
    unnamed x1, local copies, waits for them, and re-layouts  5.35 us
    mul x1, local copies, waits for them, and re-layouts, per_device(): updated * lax.rsqrt(row_power / (updated.shape[1] * lax.axis_size('col'))...  5.34 us
    mul x1, other arithmetic, per_device(): updated * lax.rsqrt(row_power / (updated.shape[1] * lax.axis_size('col'))...  4.98 us
  transfers between devices with their start and end apart: 2, of which 2 were waited for; matrix products, arithmetic and copies ran while one was open for 7% of the time, Pallas kernels for 0%

profile of v1, /device:TPU:0, one launch (start us, length us, event | category | flops | bytes accessed | tf_op | source)
XLA Modules:
  0.0 169.4 jit_solution(16390551507384613821)
XLA Ops:
  6.5 0.0 all-gather.6.cloned.1.call-start
  6.5 0.8 dynamic_slice.3
  7.3 2.0 %multiply_convert_fusion = bf16[1024,256]{1,0:T(8,128)(2,1)} fusion(bf16[1024,256]{1,0:T(8,128)(2,1)} %param.4, f32[256]{0:T(256)S(1)} %dynamic_slice.3), kind=kLoop, calls=%fused_computation.3 | loop fusion | flops 786432 | bytes 1049600 | tf_op jit(solution)/shard_map/convert_element_type | solution.py:19
  9.3 0.0 all-gather.6.cloned.1.call-update
  9.3 0.0 all-gather.4.cloned.1.call-start
  9.4 0.7 all-gather.4.cloned.1.call-update
  10.1 5.3 %copy.10 = f32[1024,1024]{0,1:T(8,128)} copy(f32[1024,1024]{1,0:T(8,128)} %param.6) | data formatting | bytes 8388608 | tf_op args[2]
  15.4 69.6 %all-gather.6.cloned.1.call-done = bf16[8192,256]{1,0:T(8,128)(2,1)} async-done(((bf16[1024,256]{1,0:T(8,128)(2,1)}), bf16[8192,256]{1,0:T(8,128)(2,1)}) %all-gather.6.cloned.1.call-update) | async-done | bytes 4194320 | tf_op jit(solution)/shard_map/all_gather | solution.py:21
  85.0 6.5 %copy.9 = bf16[1024,8,256]{0,2,1:T(8,128)(2,1)} copy(bf16[1024,8,256]{2,0,1:T(8,128)(2,1)} %bitcast.6) | data formatting | bytes 8388608 | tf_op jit(solution)/shard_map/reshape | solution.py:21
  91.5 28.1 %all-gather.4.cloned.1.call-done = bf16[2048,1024]{1,0:T(8,128)(2,1)} async-done(((bf16[512,1024]{1,0:T(8,128)(2,1)}), bf16[2048,1024]{1,0:T(8,128)(2,1)}) %all-gather.4.cloned.1.call-update) | async-done | bytes 4194320 | tf_op jit(solution)/shard_map/all_gather | solution.py:8
  119.6 11.3 %multiply_reduce_fusion = (f32[1024]{0:T(1024)S(1)}, f32[1024,1024]{0,1:T(8,128)}) fusion(f32[1024,1024]{0,1:T(8,128)} %copy.10, bf16[1024,2048]{0,1:T(8,128)(2,1)} %bitcast.7, bf16[2048,1024]{1,0:T(8,128)(2,1)} %all-gather.4.cloned.1.call-done), kind=kOutput, calls=%fused_computation | convolution fusion | flops 4298112000 | bytes 16781312 | tf_op jit(solution)/shard_map/dot_general | solution.py:13
  130.9 21.3 %psum.7 = f32[1024]{0:T(1024)S(1)} all-reduce(f32[1024]{0:T(1024)S(1)} %get-tuple-element.5), channel_id=1, replica_groups=mesh['row'=4,'col'=8] {'col'}, use_global_device_ids=true, to_apply=%region_1.0 | all-reduce | flops 1024 | bytes 8192 | tf_op jit(solution)/shard_map/psum | solution.py:29
  152.3 5.0 %broadcast_multiply_fusion = f32[1024,1024]{0,1:T(8,128)} fusion(f32[1024,1024]{0,1:T(8,128)} %get-tuple-element.6, f32[1024]{0:T(1024)S(1)} %add_rsqrt_fusion), kind=kLoop, calls=%fused_computation.1 | loop fusion | flops 1048576 | bytes 8392704 | tf_op jit(solution)/shard_map/mul | solution.py:31
  157.2 5.3 %copy.11 = f32[1024,1024]{1,0:T(8,128)} copy(f32[1024,1024]{0,1:T(8,128)} %broadcast_multiply_fusion) | data formatting | bytes 8388608 | tf_op jit(solution)/shard_map/mul | solution.py:31
  (1 shorter events, 0.0 us)
Async XLA Ops:
  6.5 78.5 %all-gather.6.cloned.1.call-start = ((), (), s32[]{:S(2)}) async-start(), calls=%async_computation.1 | async-start | bytes 4718592 | tf_op jit(solution)/shard_map/all_gather | solution.py:21
  9.3 110.3 %all-gather.4.cloned.1.call-start = ((), (), s32[]{:S(2)}) async-start(), calls=%async_computation | async-start | bytes 5242880 | tf_op jit(solution)/shard_map/all_gather | solution.py:8
Sparse Core Ops, SparseCore 0:
  9.5 75.5 all-gather.5
  86.6 32.9 all-gather.3

commit v2 on v0

--- a/solution.py
+++ b/solution.py
@@ -26,7 +26,7 @@
 
     total = taken_in(right_factor, "row", 0, take_rows, begin)
     updated = matrix - total
-    row_power = lax.psum(jnp.sum(updated * updated, axis=1), "col")
+    row_power = jnp.sum(lax.all_gather(jnp.sum(updated * updated, axis=1), "col"), axis=0)
     updated = (
         updated * lax.rsqrt(row_power / (updated.shape[1] * lax.axis_size("col")) + 1e-06)[:, None]
     )

time: 170 us -> 182 us (1.071)
  blocking collectives: 18.6 us -> 30.6 us
    all_gather x0 -> x1, blocking collectives: none -> 30.6 us  [per_device(): lax.all_gather(jnp.sum(updated * updated, axis=1), 'col')]
    psum x1 -> x0, blocking collectives: 18.6 us -> none  [per_device(): row_power = lax.psum(jnp.sum(updated * updated, axis=1), 'col')]
  transfers between devices with their start and end apart: 2 -> 2, of which waited for: 2 -> 2; matrix products, arithmetic and copies ran while one was open for 5% -> 4% of each run, Pallas kernels for 0% -> 0%
where the time goes in v2:
time: 182 us
  waiting for transfers between devices  108 us (59%)
  blocking collectives  30.6 us (17%)
  between operations  13.4 us (7%)
  local copies, waits for them, and re-layouts  11.5 us (6%)
  matrix products  11.3 us (6%)
  other arithmetic  6.99 us (4%)
    all_gather x1, waiting for transfers between devices, per_device(): left_line = lax.all_gather(scaled_left, 'col', axis=1, tiled=True)  76.7 us
    all_gather x1, waiting for transfers between devices, taken_in(): lax.all_gather(a, axis, axis=dim, tiled=True)  30.7 us
    all_gather x1, blocking collectives, per_device(): lax.all_gather(jnp.sum(updated * updated, axis=1), 'col')  30.6 us
    dot_general x1, matrix products, join_panel(): jnp.dot(left_panel, right_panel, preferred_element_type=jnp.float32)  11.3 us
    unnamed x1, local copies, waits for them, and re-layouts  5.35 us
    mul x1, local copies, waits for them, and re-layouts, per_device(): updated * lax.rsqrt(row_power / (updated.shape[1] * lax.axis_size('col'))...  5.34 us
    mul x1, other arithmetic, per_device(): updated * lax.rsqrt(row_power / (updated.shape[1] * lax.axis_size('col'))...  4.98 us
  transfers between devices with their start and end apart: 2, of which 2 were waited for; matrix products, arithmetic and copies ran while one was open for 4% of the time, Pallas kernels for 0%

profile of v2, /device:TPU:0, one launch (start us, length us, event | category | flops | bytes accessed | tf_op | source)
XLA Modules:
  0.0 181.9 jit_solution(1931856246170519597)
XLA Ops:
  6.5 0.0 all-gather.6.cloned.1.call-start
  6.5 0.7 all-gather.6.cloned.1.call-update
  7.3 0.0 all-gather.4.cloned.1.call-start
  7.3 0.8 dynamic_slice.3
  8.1 2.0 %multiply_convert_fusion = bf16[1024,256]{1,0:T(8,128)(2,1)} fusion(bf16[1024,256]{1,0:T(8,128)(2,1)} %param.4, f32[256]{0:T(256)S(1)} %dynamic_slice.3), kind=kLoop, calls=%fused_computation.3 | loop fusion | flops 786432 | bytes 1049600 | tf_op jit(solution)/shard_map/convert_element_type | solution.py:19
  10.1 0.0 all-gather.4.cloned.1.call-update
  10.1 5.3 %copy.9 = f32[1024,1024]{0,1:T(8,128)} copy(f32[1024,1024]{1,0:T(8,128)} %param.6) | data formatting | bytes 8388608 | tf_op args[2]
  15.4 30.7 %all-gather.6.cloned.1.call-done = bf16[2048,1024]{1,0:T(8,128)(2,1)} async-done(((bf16[512,1024]{1,0:T(8,128)(2,1)}), bf16[2048,1024]{1,0:T(8,128)(2,1)}) %all-gather.6.cloned.1.call-update) | async-done | bytes 4194320 | tf_op jit(solution)/shard_map/all_gather | solution.py:8
  46.1 76.7 %all-gather.4.cloned.1.call-done = bf16[1024,2048]{1,0:T(8,128)(2,1)} async-done(((bf16[1024,256]{1,0:T(8,128)(2,1)}), bf16[1024,2048]{1,0:T(8,128)(2,1)}) %all-gather.4.cloned.1.call-update) | async-done | bytes 4194320 | tf_op jit(solution)/shard_map/all_gather | solution.py:21
  122.8 11.3 %multiply_reduce_fusion = (f32[1024]{0:T(1024)S(1)}, f32[1024,1024]{0,1:T(8,128)}) fusion(f32[1024,1024]{0,1:T(8,128)} %copy.9, bf16[1024,2048]{1,0:T(8,128)(2,1)} %all-gather.4.cloned.1.call-done, bf16[2048,1024]{1,0:T(8,128)(2,1)} %all-gather.6.cloned.1.call-done), kind=kOutput, calls=%fused_computation | convolution fusion | flops 4298112000 | bytes 16781312 | tf_op jit(solution)/shard_map/dot_general | solution.py:13
  134.1 30.6 %all-gather = f32[8192]{0:T(1024)S(1)} all-gather(f32[1024]{0:T(1024)S(1)} %get-tuple-element.5), channel_id=2, replica_groups=mesh['row'=4,'col'=8] {'col'}, dimensions={0}, use_global_device_ids=true | all-gather | bytes 36864 | tf_op jit(solution)/shard_map/all_gather | solution.py:29
  164.8 5.0 %broadcast_multiply_fusion = f32[1024,1024]{0,1:T(8,128)} fusion(f32[1024,1024]{0,1:T(8,128)} %get-tuple-element.6, f32[1024]{0:T(1024)S(1)} %add_rsqrt_fusion), kind=kLoop, calls=%fused_computation.1 | loop fusion | flops 1048576 | bytes 8392704 | tf_op jit(solution)/shard_map/mul | solution.py:31
  169.8 5.3 %copy.10 = f32[1024,1024]{1,0:T(8,128)} copy(f32[1024,1024]{0,1:T(8,128)} %broadcast_multiply_fusion) | data formatting | bytes 8388608 | tf_op jit(solution)/shard_map/mul | solution.py:31
  (3 shorter events, 0.0 us)
Async XLA Ops:
  6.5 39.6 %all-gather.6.cloned.1.call-start = ((), (), s32[]{:S(2)}) async-start(), calls=%async_computation.1 | async-start | bytes 5242880 | tf_op jit(solution)/shard_map/all_gather | solution.py:8
  7.3 115.6 %all-gather.4.cloned.1.call-start = ((), (), s32[]{:S(2)}) async-start(), calls=%async_computation | async-start | bytes 4718592 | tf_op jit(solution)/shard_map/all_gather | solution.py:21
Sparse Core Ops, SparseCore 0:
  8.9 37.1 all-gather.5
  48.1 74.6 all-gather.3
